TPU v7x, 32 devices: a whole 2x2x4 slice. The times are simulated.
32 devices in a mesh: cp: 16 (over z, y, core), vocab: 2 (over x).
Axes of the slice: x: 2, y: 2, z: 4, core: 2. Of those that a mesh axis runs over, the one named last changes fastest.
Arguments:
- queries: bfloat16 [2048, 4096], P('cp', 'vocab'), may hold values from -160 to 160
- key_states: bfloat16 [2048, 1024], P('cp', 'vocab'), may hold values from -6 to 6
- value_states: bfloat16 [2048, 1024], P('cp', 'vocab'), may hold values from -6 to 6
- out_grad: bfloat16 [2048, 4096], P('cp', 'vocab'), may hold values from -6 to 6
- o_weight: bfloat16 [4096, 4096], P('vocab'), may hold values from -0.09375 to 0.09375
- span_order: int32 [32], replicated, may hold values from 0 to 31, each once
Outputs:
- query_grad: float32 [2048, 4096], P('cp', 'vocab')
- key_grad: float32 [2048, 1024], P('cp', 'vocab')
- value_grad: float32 [2048, 1024], P('cp', 'vocab')
Inputs may be any that keep to these rules, and one draw needn't show every extreme that they name: `span_order`: each of the 32 span indices once.
All inputs are finite; a program needn't handle non-finite values.
Results may differ from a plain program's by a relative error of at most 0.014.
Values may be sent and summed in bfloat16 or wider, within the bound.
A program may use at most 64 MiB of HBM per device.

v0:
```python
import jax
import jax.numpy as jnp
from jax import lax
from jax.sharding import PartitionSpec as P

HEADS = 32
KV_HEADS = 8
HEAD_DIM = 128


def positions(span_order, span_rows):
    offsets = jnp.arange(span_rows, dtype=jnp.int32)
    return (span_order[:, None] * span_rows + offsets[None, :]).reshape(-1)


def block_scores(query_block, key_block, query_places, key_places, factor):
    scores = (
        jnp.einsum("qkgd,skd->kgqs", query_block, key_block, preferred_element_type=jnp.float32)
        * factor
    )
    visible = key_places[None, :] <= query_places[:, None]
    return jnp.where(visible, scores, -jnp.inf)


def local(queries, key_states, value_states, out_grad, o_weight, span_order):
    own_rows = queries.shape[0]
    kv_width = key_states.shape[1]
    kv_heads = kv_width // HEAD_DIM
    groups = HEADS // KV_HEADS
    factor = HEAD_DIM ** (-0.5)
    upstream = lax.dot_general(
        lax.all_gather(out_grad, "vocab", axis=1, tiled=True),
        o_weight,
        (((1,), (1,)), ((), ())),
        preferred_element_type=jnp.float32,
    ).astype(jnp.bfloat16)
    places = positions(span_order, own_rows // 2)
    seq_len = places.shape[0]
    own_places = lax.dynamic_slice_in_dim(places, lax.axis_index("cp") * own_rows, own_rows, 0)
    query_heads = queries.reshape(own_rows, kv_heads, groups, HEAD_DIM)
    upstream_heads = upstream.reshape(own_rows, kv_heads, groups, HEAD_DIM)
    key_all, value_all = (
        lax.all_gather(key_states, "cp", axis=0, tiled=True),
        lax.all_gather(value_states, "cp", axis=0, tiled=True),
    )
    key_all = key_all.reshape(seq_len, kv_heads, HEAD_DIM)
    value_all = value_all.reshape(seq_len, kv_heads, HEAD_DIM)
    block_rows = own_rows * 8
    block_count = seq_len // block_rows
    block_ids = jnp.arange(block_count, dtype=jnp.int32)
    stat_shape = (kv_heads, groups, own_rows)

    def key_block(block_index):
        offset = block_index * block_rows
        return (
            lax.dynamic_slice_in_dim(key_all, offset, block_rows, 0),
            lax.dynamic_slice_in_dim(value_all, offset, block_rows, 0),
            lax.dynamic_slice_in_dim(places, offset, block_rows, 0),
        )

    def stats_step(carried, block_index):
        running, totals, delta_acc = carried
        keys_now, values_now, places_now = key_block(block_index)
        scores = block_scores(query_heads, keys_now, own_places, places_now, factor)
        newest = jnp.maximum(running, jnp.max(scores, axis=3))
        rescale = jnp.exp(running - newest)
        raised = jnp.exp(scores - newest[..., None])
        grad_probs = jnp.einsum(
            "qkgd,skd->kgqs", upstream_heads, values_now, preferred_element_type=jnp.float32
        )
        totals = totals * rescale + jnp.sum(raised, axis=3)
        delta_acc = delta_acc * rescale + jnp.sum(raised * grad_probs, axis=3)
        return ((newest, totals, delta_acc), None)

    start_stats = (
        jnp.full(stat_shape, -1e30, jnp.float32),
        jnp.zeros(stat_shape, jnp.float32),
        jnp.zeros(stat_shape, jnp.float32),
    )
    (running, totals, delta_acc), unused = lax.scan(stats_step, start_stats, block_ids)
    logsum = running + jnp.log(totals)
    deltas = delta_acc / totals

    def grad_pieces(block_index):
        keys_now, values_now, places_now = key_block(block_index)
        scores = block_scores(query_heads, keys_now, own_places, places_now, factor)
        weights = jnp.exp(scores - logsum[..., None])
        grad_probs = jnp.einsum(
            "qkgd,skd->kgqs", upstream_heads, values_now, preferred_element_type=jnp.float32
        )
        grad_scores = (weights * (grad_probs - deltas[..., None])).astype(jnp.bfloat16)
        return (keys_now, weights, grad_scores)

    query_zeros = jnp.zeros((own_rows, kv_heads, groups, HEAD_DIM), jnp.float32)

    def grad_step(carried, block_index):
        keys_now, weights, grad_scores = grad_pieces(block_index)
        carried = (
            carried
            + jnp.einsum(
                "kgqs,skd->qkgd", grad_scores, keys_now, preferred_element_type=jnp.float32
            )
            * factor
        )
        key_term = (
            jnp.einsum(
                "kgqs,qkgd->skd", grad_scores, query_heads, preferred_element_type=jnp.float32
            )
            * factor
        )
        value_term = jnp.einsum(
            "kgqs,qkgd->skd",
            weights.astype(jnp.bfloat16),
            upstream_heads,
            preferred_element_type=jnp.float32,
        )
        joined = jnp.concatenate(
            (key_term.reshape(block_rows, kv_width), value_term.reshape(block_rows, kv_width)),
            axis=1,
        )
        return (carried, joined)

    query_total, stacked = lax.scan(grad_step, query_zeros, block_ids)
    terms = stacked.reshape(seq_len, 2 * kv_width)
    mine = lax.psum_scatter(
        terms.astype(jnp.bfloat16), "cp", scatter_dimension=0, tiled=True
    ).astype(jnp.float32)
    key_grad = mine[:, :kv_width]
    value_grad = mine[:, kv_width:]
    query_grad = query_total.reshape(own_rows, kv_heads * groups * HEAD_DIM)
    return (query_grad, key_grad, value_grad)


def solution(mesh):
    return jax.shard_map(
        local,
        mesh=mesh,
        in_specs=(
            P("cp", "vocab"),
            P("cp", "vocab"),
            P("cp", "vocab"),
            P("cp", "vocab"),
            P("vocab", None),
            P(),
        ),
        out_specs=(P("cp", "vocab"), P("cp", "vocab"), P("cp", "vocab")),
        check_vma=False,
    )
```

profile of v0, /device:TPU:0, one launch (start us, length us, event | category | flops | bytes accessed | tf_op | source)
XLA Modules:
  0.0 253.9 jit_solution(16052969904517764224)
XLA Ops:
  7.9 1.7 copy.27
  9.7 1.7 copy.29
  12.3 1.3 copy.28
  14.7 18.9 %all-gather.8.cloned.1.call-done = bf16[128,4096]{1,0:T(8,128)(2,1)} async-done(((bf16[128,2048]{1,0:T(8,128)(2,1)}), bf16[128,4096]{1,0:T(8,128)(2,1)}) %all-gather.8.cloned.1.call-update) | async-done | bytes 1048592 | tf_op jit(solution)/shard_map/all_gather | solution.py:32
  33.6 11.8 %convolution_convert_fusion = bf16[128,2048]{1,0:T(8,128)(2,1)S(1)} fusion(bf16[128,4096]{1,0:T(8,128)(2,1)} %all-gather.8.cloned.1.call-done, bf16[2048,4096]{1,0:T(8,128)(2,1)} %param.14), kind=kOutput, calls=%fused_computation.51 | convolution fusion | flops 2147745792 | bytes 18350080 | tf_op jit(solution)/shard_map/dot_general | solution.py:31
  46.7 1.3 copy.36
  47.9 29.4 %all-gather.4.cloned.1.call-done = bf16[2048,512]{0,1:T(8,128)(2,1)} async-done(((bf16[128,512]{0,1:T(8,128)(2,1)}), bf16[2048,512]{0,1:T(8,128)(2,1)}) %all-gather.4.cloned.1.call-update) | async-done | bytes 2097168 | tf_op jit(solution)/shard_map/all_gather | solution.py:43
  77.4 3.0 %copy.34 = bf16[2048,4,128]{2,0,1:T(8,128)(2,1)S(1)} copy(bf16[2048,4,128]{0,2,1:T(8,128)(2,1)} %bitcast.158) | data formatting | bytes 4194304
  80.4 39.9 %all-gather.6.cloned.1.call-done = bf16[2048,512]{0,1:T(8,128)(2,1)} async-done(((bf16[128,512]{0,1:T(8,128)(2,1)}), bf16[2048,512]{0,1:T(8,128)(2,1)}) %all-gather.6.cloned.1.call-update) | async-done | bytes 2097168 | tf_op jit(solution)/shard_map/all_gather | solution.py:44
  120.2 4.0 %copy.32 = bf16[2048,4,128]{2,0,1:T(8,128)(2,1)} copy(bf16[2048,4,128]{0,2,1:T(8,128)(2,1)} %bitcast.159) | data formatting | bytes 4194304
  124.2 16.3 %while.28 = (s32[]{:T(128)}, f32[4,4,128]{2,1,0:T(4,128)S(1)}, f32[4,4,128]{2,1,0:T(4,128)S(1)}, f32[4,4,128]{2,1,0:T(4,128)S(1)}, s32[2]{0:T(128)S(1)}, /*index...) while((s32[]{:T(128)}, f32[4,4,128]{2,1,0:T(4,128)S(1)}, ...), condition=%wide.region_4.5_spmd.clone, body=%wide.region_0.4_spmd.clone.sunk | while | flops 1099053056 | bytes 39482140 | solution.py:80
  125.7 2.4 fusion.75
  128.2 2.5 fusion.76
  130.6 1.7 fusion.77
  133.9 2.4 fusion.75
  136.4 2.4 fusion.76
  138.8 1.7 fusion.77
  140.6 26.7 %while.29 = (s32[]{:T(128)}, f32[128,4,4,128]{0,3,2,1:T(8,128)S(1)}, bf16[2,1024,1024]{1,2,0:T(8,128)(2,1)}, s32[2]{0:T(128)S(1)}, bf16[2048,4,128]{2,0,1:T(8,12...) while((s32[]{:T(128)}, ...), condition=%wide.region_6.7_spmd.clone, body=%wide.region_5.6_spmd.clone.sunk | while | flops 2711486464 | bytes 97948544 | solution.py:123
  142.1 2.3 fusion.89
  144.4 2.1 fusion.92
  146.6 2.5 fusion.90
  150.2 1.5 bitcast_multiply_fusion.3
  152.0 1.9 copy-done.3
  155.4 2.3 fusion.89
  157.7 2.1 fusion.92
  159.9 2.5 fusion.90
  163.5 1.5 bitcast_multiply_fusion.3
  165.3 1.9 copy-done.3
  167.3 6.2 %copy.38 = bf16[2,1024,1024]{2,1,0:T(8,128)(2,1)} copy(bf16[2,1024,1024]{1,2,0:T(8,128)(2,1)} %get-tuple-element.129) | data formatting | bytes 8388608 | tf_op jit(solution)/shard_map/convert_element_type | solution.py:126
  173.5 1.3 copy.51
  174.8 70.7 %reduce-scatter.2.cloned.1.call-done = bf16[128,1024]{1,0:T(8,128)(2,1)} async-done(((bf16[2048,1024]{1,0:T(8,128)(2,1)}), bf16[128,1024]{1,0:T(8,128)(2,1)}) %reduce-scatter.2.cloned.1.call-update) | async-done | bytes 262160 | tf_op jit(solution)/shard_map/reduce_scatter | solution.py:125
  245.5 1.8 fusion.38
  (73 shorter events, 10.1 us)
Async XLA Ops:
  7.2 26.4 %all-gather.8.cloned.1.call-start = ((), (), s32[]{:S(2)}) async-start(), calls=%async_computation.3 | async-start | bytes 1572864 | tf_op jit(solution)/shard_map/all_gather | solution.py:32
  7.9 69.5 %all-gather.4.cloned.1.call-start = ((), (), s32[]{:S(2)}) async-start(), calls=%async_computation.1 | async-start | bytes 2228224 | tf_op jit(solution)/shard_map/all_gather | solution.py:43
  9.6 110.6 %all-gather.6.cloned.1.call-start = ((), (), s32[]{:S(2)}) async-start(), calls=%async_computation.2 | async-start | bytes 2228224 | tf_op jit(solution)/shard_map/all_gather | solution.py:44
  11.4 234.1 %reduce-scatter.2.cloned.1.call-start = ((), (), s32[]{:S(2)}) async-start(), calls=%async_computation.4 | async-start | bytes 4456448 | tf_op jit(solution)/shard_map/reduce_scatter | solution.py:125
  13.6 31.7 %copy-start = (bf16[128,2048]{0,1:T(8,128)(2,1)}, bf16[128,2048]{0,1:T(8,128)(2,1)S(1)}, u32[]{:S(2)}) copy-start(bf16[128,2048]{0,1:T(8,128)(2,1)S(1)} %copy.28) | copy-start | bytes 1572868
  125.4 2.7 %copy-start.4 = (bf16[2048,4,128]{2,0,1:T(8,128)(2,1)S(1)}, bf16[2048,4,128]{2,0,1:T(8,128)(2,1)}, u32[]{:S(2)}) copy-start(bf16[2048,4,128]{2,0,1:T(8,128)(2,1)} %get-tuple-element.494) | copy-start | bytes 6291460 | tf_op jit(solution)/shard_map/while
  125.5 2.7 %copy-start.7 = (bf16[128,4,4,128]{3,0,2,1:T(8,128)(2,1)S(1)}, bf16[128,4,4,128]{3,0,2,1:T(8,128)(2,1)}, u32[]{:S(2)}) copy-start(bf16[128,4,4,128]{3,0,2,1:T(8,128)(2,1)} %get-tuple-element.495) | copy-start | bytes 1572868 | tf_op jit(solution)/shard_map/while
  133.6 2.7 %copy-start.4 = (bf16[2048,4,128]{2,0,1:T(8,128)(2,1)S(1)}, bf16[2048,4,128]{2,0,1:T(8,128)(2,1)}, u32[]{:S(2)}) copy-start(bf16[2048,4,128]{2,0,1:T(8,128)(2,1)} %get-tuple-element.494) | copy-start | bytes 6291460 | tf_op jit(solution)/shard_map/while
  133.6 2.7 %copy-start.7 = (bf16[128,4,4,128]{3,0,2,1:T(8,128)(2,1)S(1)}, bf16[128,4,4,128]{3,0,2,1:T(8,128)(2,1)}, u32[]{:S(2)}) copy-start(bf16[128,4,4,128]{3,0,2,1:T(8,128)(2,1)} %get-tuple-element.495) | copy-start | bytes 1572868 | tf_op jit(solution)/shard_map/while
  141.8 2.5 copy-start.6
  144.4 2.2 copy-start.5
  146.5 3.6 %copy-start.1 = (bf16[128,4,4,128]{0,3,2,1:T(8,128)(2,1)S(1)}, bf16[128,4,4,128]{0,3,2,1:T(8,128)(2,1)}, u32[]{:S(2)}) copy-start(bf16[128,4,4,128]{0,3,2,1:T(8,128)(2,1)} %get-tuple-element.539) | copy-start | bytes 1572868 | tf_op jit(solution)/shard_map/while
  149.1 2.6 %copy-start.2 = (bf16[2,1024,1024]{1,2,0:T(8,128)(2,1)S(1)}, bf16[2,1024,1024]{1,2,0:T(8,128)(2,1)}, u32[]{:S(2)}) copy-start(bf16[2,1024,1024]{1,2,0:T(8,128)(2,1)} %get-tuple-element.518) | copy-start | bytes 12582916 | tf_op jit(solution)/shard_map/while
  152.0 1.9 copy-start.3
  155.2 2.5 copy-start.6
  157.7 2.2 copy-start.5
  159.9 3.6 %copy-start.1 = (bf16[128,4,4,128]{0,3,2,1:T(8,128)(2,1)S(1)}, bf16[128,4,4,128]{0,3,2,1:T(8,128)(2,1)}, u32[]{:S(2)}) copy-start(bf16[128,4,4,128]{0,3,2,1:T(8,128)(2,1)} %get-tuple-element.539) | copy-start | bytes 1572868 | tf_op jit(solution)/shard_map/while
  162.4 2.6 %copy-start.2 = (bf16[2,1024,1024]{1,2,0:T(8,128)(2,1)S(1)}, bf16[2,1024,1024]{1,2,0:T(8,128)(2,1)}, u32[]{:S(2)}) copy-start(bf16[2,1024,1024]{1,2,0:T(8,128)(2,1)} %get-tuple-element.518) | copy-start | bytes 12582916 | tf_op jit(solution)/shard_map/while
  165.3 1.9 copy-start.3
Sparse Core Ops, SparseCore 0:
  9.5 23.9 all-gather.7
  36.3 41.0 all-gather.3
  80.1 40.1 all-gather.5
  173.6 71.8 reduce-scatter.1
where the time goes:
time: 254 us
  waiting for transfers between devices  160 us (63%)
  matrix products  40.6 us (16%)
  local copies, waits for them, and re-layouts  31.1 us (12%)
  between operations  13.9 us (5%)
  other arithmetic  5.53 us (2%)
  loops' own time  3.08 us (1%)
    reduce_scatter x1, waiting for transfers between devices, local(): lax.psum_scatter(terms.astype(jnp.bfloat16), 'cp', scatter_dimension=0, t...  70.7 us
    all_gather x1, waiting for transfers between devices, local(): lax.all_gather(value_states, 'cp', axis=0, tiled=True)  39.9 us
    all_gather x1, waiting for transfers between devices, local(): lax.all_gather(key_states, 'cp', axis=0, tiled=True)  29.4 us
    all_gather x1, waiting for transfers between devices, local(): lax.all_gather(out_grad, 'vocab', axis=1, tiled=True)  18.9 us
    unnamed x10, local copies, waits for them, and re-layouts  14.9 us
    dot_general x1, matrix products, local(): lax.dot_general(lax.all_gather(out_grad, 'vocab', axis=1, tiled=True), o_...  11.8 us
    dot_general x4, matrix products, block_scores(): jnp.einsum('qkgd,skd->kgqs', query_block, key_block, preferred_element_ty...  9.46 us
    convert_element_type x1, local copies, waits for them, and re-layouts, local(): terms.astype(jnp.bfloat16)  6.24 us
  transfers between devices with their start and end apart: 4, of which 4 were waited for; matrix products, arithmetic and copies ran while one was open for 10% of the time, Pallas kernels for 0%

commit v1 on v0

--- a/solution.py
+++ b/solution.py
@@ -40,7 +40,9 @@
     query_heads = queries.reshape(own_rows, kv_heads, groups, HEAD_DIM)
     upstream_heads = upstream.reshape(own_rows, kv_heads, groups, HEAD_DIM)
     key_all, value_all = (
-        lax.all_gather(key_states, "cp", axis=0, tiled=True),
+        jnp.concatenate(
+            lax.all_to_all(jnp.stack([key_states] * lax.axis_size("cp")), "cp", 0, 0), axis=0
+        ),
         lax.all_gather(value_states, "cp", axis=0, tiled=True),
     )
     key_all = key_all.reshape(seq_len, kv_heads, HEAD_DIM)

time: 254 us -> 230 us (0.906)
  waiting for transfers between devices: 160 us -> 121 us
  starting transfers between devices: 0.16 us -> 7.58 us
  local copies, waits for them, and re-layouts: 31.1 us -> 37.4 us
    all_gather x1 -> x0, waiting for transfers between devices: 29.4 us -> none  [local(): lax.all_gather(key_states, 'cp', axis=0, tiled=True)]
    all_gather x1, waiting for transfers between devices: 18.9 us -> 10.3 us  [local(): lax.all_gather(out_grad, 'vocab', axis=1, tiled=True)]
    all_to_all x0 -> x1, starting transfers between devices: none -> 7.46 us  [local(): lax.all_to_all(jnp.stack([key_states] * lax.axis_size('cp')), 'cp', 0, 0)]
    another operation x0 -> x2, local copies, waits for them, and re-layouts: none -> 4.08 us  [the longest x1 2.33 us: local(): key_all = key_all.reshape(seq_len, kv_heads, HEAD_DIM)]
    all_to_all x0 -> x1, local copies, waits for them, and re-layouts: none -> 2.94 us  [local(): lax.all_to_all(jnp.stack([key_states] * lax.axis_size('cp')), 'cp', 0, 0)]
  transfers between devices with their start and end apart: 4 -> 4, of which waited for: 4 -> 3; matrix products, arithmetic and copies ran while one was open for 10% -> 12% of each run, Pallas kernels for 0% -> 0%
where the time goes in v1:
time: 230 us; the launch traced here: 229 us
  waiting for transfers between devices  121 us (53%)
  matrix products  40.6 us (18%)
  local copies, waits for them, and re-layouts  37.4 us (16%)
  between operations  13.9 us (6%)
  starting transfers between devices  7.58 us (3%)
  other arithmetic  5.54 us (2%)
  loops' own time  3.28 us (1%)
    reduce_scatter x1, waiting for transfers between devices, local(): lax.psum_scatter(terms.astype(jnp.bfloat16), 'cp', scatter_dimension=0, t...  70.6 us
    all_gather x1, waiting for transfers between devices, local(): lax.all_gather(value_states, 'cp', axis=0, tiled=True)  39.2 us
    unnamed x10, local copies, waits for them, and re-layouts  14.2 us
    dot_general x1, matrix products, local(): lax.dot_general(lax.all_gather(out_grad, 'vocab', axis=1, tiled=True), o_...  11.8 us
    all_gather x1, waiting for transfers between devices, local(): lax.all_gather(out_grad, 'vocab', axis=1, tiled=True)  10.3 us
    dot_general x4, matrix products, block_scores(): jnp.einsum('qkgd,skd->kgqs', query_block, key_block, preferred_element_ty...  9.46 us
    all_to_all x1, starting transfers between devices, local(): lax.all_to_all(jnp.stack([key_states] * lax.axis_size('cp')), 'cp', 0, 0)  7.46 us
    convert_element_type x1, local copies, waits for them, and re-layouts, local(): terms.astype(jnp.bfloat16)  6.23 us
  transfers between devices with their start and end apart: 4, of which 3 were waited for; matrix products, arithmetic and copies ran while one was open for 12% of the time, Pallas kernels for 0%

profile of v1, /device:TPU:0, one launch (start us, length us, event | category | flops | bytes accessed | tf_op | source)
XLA Modules:
  0.0 229.1 jit_solution(10056433214175790594)
XLA Ops:
  7.9 1.7 copy.48
  10.7 1.7 stack.2
  12.4 7.5 %all-to-all-start = ((bf16[16,128,512]{1,2,0:T(8,128)(2,1)}), bf16[16,128,512]{1,2,0:T(8,128)(2,1)}, u32[]{:S(2)}, u32[]{:S(2)}) async-start(bf16[16,128,512]{1,2,0:T(8,128)(2,1)} %stack.2), calls=%async_computation | async-start | bytes 4194304 | tf_op jit(solution)/shard_map/all_to_all | solution.py:44
  20.8 1.3 copy.47
  23.2 10.3 %all-gather.5.cloned.1.call-done = bf16[128,4096]{1,0:T(8,128)(2,1)} async-done(((bf16[128,2048]{1,0:T(8,128)(2,1)}), bf16[128,4096]{1,0:T(8,128)(2,1)}) %all-gather.5.cloned.1.call-update) | async-done | bytes 1048592 | tf_op jit(solution)/shard_map/all_gather | solution.py:32
  33.6 11.8 %convolution_convert_fusion = bf16[128,2048]{1,0:T(8,128)(2,1)S(1)} fusion(bf16[128,4096]{1,0:T(8,128)(2,1)} %all-gather.5.cloned.1.call-done, bf16[2048,4096]{1,0:T(8,128)(2,1)} %param.14), kind=kOutput, calls=%fused_computation.51 | convolution fusion | flops 2147745792 | bytes 18350080 | tf_op jit(solution)/shard_map/dot_general | solution.py:31
  47.9 39.2 %all-gather.3.cloned.1.call-done = bf16[2048,512]{0,1:T(8,128)(2,1)} async-done(((bf16[128,512]{0,1:T(8,128)(2,1)}), bf16[2048,512]{0,1:T(8,128)(2,1)}) %all-gather.3.cloned.1.call-update) | async-done | bytes 2097168 | tf_op jit(solution)/shard_map/all_gather | solution.py:46
  87.1 3.9 %copy.51 = bf16[2048,4,128]{2,0,1:T(8,128)(2,1)} copy(bf16[2048,4,128]{0,2,1:T(8,128)(2,1)} %bitcast.159) | data formatting | bytes 4194304
  91.0 2.9 %copy.46 = bf16[16,128,512]{1,0,2:T(8,128)(2,1)S(1)} copy(bf16[16,128,512]{1,2,0:T(8,128)(2,1)} %all-to-all-done) | data formatting | bytes 4194304 | tf_op jit(solution)/shard_map/all_to_all | solution.py:44
  94.0 2.3 %reshape_reshape.3 = bf16[2048,4,128]{0,2,1:T(8,128)(2,1)} reshape(bf16[16,128,512]{1,0,2:T(8,128)(2,1)S(1)} %copy.46) | data formatting | bytes 4194304 | tf_op jit(solution)/shard_map/reshape;reshape | solution.py:48
  96.3 3.0 %copy.53 = bf16[2048,4,128]{2,0,1:T(8,128)(2,1)S(1)} copy(bf16[2048,4,128]{0,2,1:T(8,128)(2,1)} %reshape_reshape.3) | data formatting | bytes 4194304
  99.4 16.4 %while.28 = (s32[]{:T(128)}, f32[4,4,128]{2,1,0:T(4,128)S(1)}, f32[4,4,128]{2,1,0:T(4,128)S(1)}, f32[4,4,128]{2,1,0:T(4,128)S(1)}, s32[2]{0:T(128)S(1)}, /*index...) while((s32[]{:T(128)}, f32[4,4,128]{2,1,0:T(4,128)S(1)}, ...), condition=%wide.region_4.5_spmd.clone, body=%wide.region_0.4_spmd.clone.sunk | while | flops 1099053056 | bytes 39482140 | solution.py:82
  100.9 2.4 %fusion.75 = (f32[4,4,128]{2,1,0:T(4,128)S(1)}, f32[4,1024,128,4]{2,1,3,0:T(8,128)S(1)}) fusion(pred[128,1024]{0,1:T(8,128)(4,1)S(1)} %broadcast_compare_fusion.4, bf16[128,4,4,128]{3,0,2,1:T(8,128)(2,1)} %get-tuple-element.516, bf16[2048,4,128]{2,0,1:T(8,128)(2,1)S(1)} %get-tuple-element.515, s32[]{:T(128)S(6)} %select_n.52), kind=kOutput, calls=%fused_computation.5.clone.1 | convolution fusion | flops 543160320 | bytes 10100740 | tf_op jit(solution)/shard_map/while/body/eval_jaxpr/qkgd,skd->kgqs/dot_general | solution.py:18
  103.3 2.5 %fusion.76 = f32[4,4,128]{2,1,0:T(4,128)S(1)} fusion(f32[4,1024,128,4]{2,1,3,0:T(8,128)S(1)} %get-tuple-element.463, f32[4,4,128]{2,1,0:T(4,128)S(1)} %select_maximum_fusion.2, pred[128,1024]{0,1:T(8,128)(4,1)S(1)} %broadcast_compare_fusion.4, bf16[128,4,4,128]{3,0,2,1:T(8,128)(2,1)S(1)} %copy-done.7, bf16[2048,4,128]{2,0,1:T(8,128)(2,1)S(1)} %copy-done.4, ...), kind=kOutput, calls=%fused_computation.1.clone.1 | convolution fusion | flops 547354624 | bytes 10108932 | tf_op jit(solution)/shard_map/while/body/eval_jaxpr/qkgd,skd->kgqs/dot_general | solution.py:70
  105.8 1.7 fusion.77
  109.0 2.4 %fusion.75 = (f32[4,4,128]{2,1,0:T(4,128)S(1)}, f32[4,1024,128,4]{2,1,3,0:T(8,128)S(1)}) fusion(pred[128,1024]{0,1:T(8,128)(4,1)S(1)} %broadcast_compare_fusion.4, bf16[128,4,4,128]{3,0,2,1:T(8,128)(2,1)} %get-tuple-element.516, bf16[2048,4,128]{2,0,1:T(8,128)(2,1)S(1)} %get-tuple-element.515, s32[]{:T(128)S(6)} %select_n.52), kind=kOutput, calls=%fused_computation.5.clone.1 | convolution fusion | flops 543160320 | bytes 10100740 | tf_op jit(solution)/shard_map/while/body/eval_jaxpr/qkgd,skd->kgqs/dot_general | solution.py:18
  111.5 2.5 %fusion.76 = f32[4,4,128]{2,1,0:T(4,128)S(1)} fusion(f32[4,1024,128,4]{2,1,3,0:T(8,128)S(1)} %get-tuple-element.463, f32[4,4,128]{2,1,0:T(4,128)S(1)} %select_maximum_fusion.2, pred[128,1024]{0,1:T(8,128)(4,1)S(1)} %broadcast_compare_fusion.4, bf16[128,4,4,128]{3,0,2,1:T(8,128)(2,1)S(1)} %copy-done.7, bf16[2048,4,128]{2,0,1:T(8,128)(2,1)S(1)} %copy-done.4, ...), kind=kOutput, calls=%fused_computation.1.clone.1 | convolution fusion | flops 547354624 | bytes 10108932 | tf_op jit(solution)/shard_map/while/body/eval_jaxpr/qkgd,skd->kgqs/dot_general | solution.py:70
  114.0 1.7 fusion.77
  115.8 26.9 %while.29 = (s32[]{:T(128)}, f32[128,4,4,128]{0,3,2,1:T(8,128)S(1)}, bf16[2,1024,1024]{1,2,0:T(8,128)(2,1)}, s32[2]{0:T(128)S(1)}, bf16[2048,4,128]{2,0,1:T(8,12...) while((s32[]{:T(128)}, ...), condition=%wide.region_6.7_spmd.clone, body=%wide.region_5.6_spmd.clone.sunk | while | flops 2711486464 | bytes 97948544 | solution.py:125
  117.4 2.3 fusion.89
  119.7 2.1 fusion.92
  121.9 2.5 %fusion.90 = bf16[4,4,128,1024]{2,3,1,0:T(8,128)(2,1)S(1)} fusion(f32[4,1024,128,4]{2,1,3,0:T(8,128)S(1)} %fusion.89, f32[4,4,128]{2,1,0:T(4,128)S(1)} %get-tuple-element.566, f32[4,4,128]{2,1,0:T(4,128)S(1)} %get-tuple-element.563, pred[128,1024]{0,1:T(8,128)(4,1)S(1)} %broadcast_compare_fusion.5, bf16[128,4,4,128]{0,3,2,1:T(8,128)(2,1)S(1)} %copy-done.6, ...), kind=kOutput, calls=%fused_computation.22.clone.1 | convolution fusion | flops 549453824 | bytes 14303236 | tf_op jit(solution)/shard_map/while/body/eval_jaxpr/qkgd,skd->kgqs/dot_general | solution.py:90
  125.6 1.5 bitcast_multiply_fusion.3
  127.4 1.9 copy-done.3
  130.8 2.3 fusion.89
  133.1 2.1 fusion.92
  135.3 2.5 %fusion.90 = bf16[4,4,128,1024]{2,3,1,0:T(8,128)(2,1)S(1)} fusion(f32[4,1024,128,4]{2,1,3,0:T(8,128)S(1)} %fusion.89, f32[4,4,128]{2,1,0:T(4,128)S(1)} %get-tuple-element.566, f32[4,4,128]{2,1,0:T(4,128)S(1)} %get-tuple-element.563, pred[128,1024]{0,1:T(8,128)(4,1)S(1)} %broadcast_compare_fusion.5, bf16[128,4,4,128]{0,3,2,1:T(8,128)(2,1)S(1)} %copy-done.6, ...), kind=kOutput, calls=%fused_computation.22.clone.1 | convolution fusion | flops 549453824 | bytes 14303236 | tf_op jit(solution)/shard_map/while/body/eval_jaxpr/qkgd,skd->kgqs/dot_general | solution.py:90
  138.9 1.5 bitcast_multiply_fusion.3
  140.7 1.9 copy-done.3
  142.6 6.2 %copy.57 = bf16[2,1024,1024]{2,1,0:T(8,128)(2,1)} copy(bf16[2,1024,1024]{1,2,0:T(8,128)(2,1)} %get-tuple-element.129) | data formatting | bytes 8388608 | tf_op jit(solution)/shard_map/convert_element_type | solution.py:128
  150.2 70.6 %reduce-scatter.2.cloned.1.call-done = bf16[128,1024]{1,0:T(8,128)(2,1)} async-done(((bf16[2048,1024]{1,0:T(8,128)(2,1)}), bf16[128,1024]{1,0:T(8,128)(2,1)}) %reduce-scatter.2.cloned.1.call-update) | async-done | bytes 262160 | tf_op jit(solution)/shard_map/reduce_scatter | solution.py:127
  220.8 1.8 fusion.38
  (75 shorter events, 13.6 us)
Async XLA Ops:
  7.2 26.4 %all-gather.5.cloned.1.call-start = ((), (), s32[]{:S(2)}) async-start(), calls=%async_computation.3 | async-start | bytes 1572864 | tf_op jit(solution)/shard_map/all_gather | solution.py:32
  7.9 79.2 %all-gather.3.cloned.1.call-start = ((), (), s32[]{:S(2)}) async-start(), calls=%async_computation.2 | async-start | bytes 2228224 | tf_op jit(solution)/shard_map/all_gather | solution.py:46
  12.4 78.6 %all-to-all-start = ((bf16[16,128,512]{1,2,0:T(8,128)(2,1)}), bf16[16,128,512]{1,2,0:T(8,128)(2,1)}, u32[]{:S(2)}, u32[]{:S(2)}) async-start(bf16[16,128,512]{1,2,0:T(8,128)(2,1)} %stack.2), calls=%async_computation | async-start | bytes 4194304 | tf_op jit(solution)/shard_map/all_to_all | solution.py:44
  19.9 200.9 %reduce-scatter.2.cloned.1.call-start = ((), (), s32[]{:S(2)}) async-start(), calls=%async_computation.4 | async-start | bytes 4456448 | tf_op jit(solution)/shard_map/reduce_scatter | solution.py:127
  22.1 23.2 %copy-start = (bf16[128,2048]{0,1:T(8,128)(2,1)}, bf16[128,2048]{0,1:T(8,128)(2,1)S(1)}, u32[]{:S(2)}) copy-start(bf16[128,2048]{0,1:T(8,128)(2,1)S(1)} %copy.47) | copy-start | bytes 1572868
  100.6 2.7 %copy-start.4 = (bf16[2048,4,128]{2,0,1:T(8,128)(2,1)S(1)}, bf16[2048,4,128]{2,0,1:T(8,128)(2,1)}, u32[]{:S(2)}) copy-start(bf16[2048,4,128]{2,0,1:T(8,128)(2,1)} %get-tuple-element.517) | copy-start | bytes 6291460 | tf_op jit(solution)/shard_map/while
  100.6 2.7 %copy-start.7 = (bf16[128,4,4,128]{3,0,2,1:T(8,128)(2,1)S(1)}, bf16[128,4,4,128]{3,0,2,1:T(8,128)(2,1)}, u32[]{:S(2)}) copy-start(bf16[128,4,4,128]{3,0,2,1:T(8,128)(2,1)} %get-tuple-element.518) | copy-start | bytes 1572868 | tf_op jit(solution)/shard_map/while
  108.8 2.7 %copy-start.4 = (bf16[2048,4,128]{2,0,1:T(8,128)(2,1)S(1)}, bf16[2048,4,128]{2,0,1:T(8,128)(2,1)}, u32[]{:S(2)}) copy-start(bf16[2048,4,128]{2,0,1:T(8,128)(2,1)} %get-tuple-element.517) | copy-start | bytes 6291460 | tf_op jit(solution)/shard_map/while
  108.8 2.7 %copy-start.7 = (bf16[128,4,4,128]{3,0,2,1:T(8,128)(2,1)S(1)}, bf16[128,4,4,128]{3,0,2,1:T(8,128)(2,1)}, u32[]{:S(2)}) copy-start(bf16[128,4,4,128]{3,0,2,1:T(8,128)(2,1)} %get-tuple-element.518) | copy-start | bytes 1572868 | tf_op jit(solution)/shard_map/while
  117.2 2.5 %copy-start.6 = (bf16[128,4,4,128]{0,3,2,1:T(8,128)(2,1)S(1)}, bf16[128,4,4,128]{0,3,2,1:T(8,128)(2,1)}, u32[]{:S(2)}) copy-start(bf16[128,4,4,128]{0,3,2,1:T(8,128)(2,1)} %get-tuple-element.565) | copy-start | bytes 1572868 | tf_op jit(solution)/shard_map/while
  119.7 2.2 copy-start.5
  121.9 3.6 %copy-start.1 = (bf16[128,4,4,128]{0,3,2,1:T(8,128)(2,1)S(1)}, bf16[128,4,4,128]{0,3,2,1:T(8,128)(2,1)}, u32[]{:S(2)}) copy-start(bf16[128,4,4,128]{0,3,2,1:T(8,128)(2,1)} %get-tuple-element.562) | copy-start | bytes 1572868 | tf_op jit(solution)/shard_map/while
  124.5 2.6 %copy-start.2 = (bf16[2,1024,1024]{1,2,0:T(8,128)(2,1)S(1)}, bf16[2,1024,1024]{1,2,0:T(8,128)(2,1)}, u32[]{:S(2)}) copy-start(bf16[2,1024,1024]{1,2,0:T(8,128)(2,1)} %get-tuple-element.541) | copy-start | bytes 12582916 | tf_op jit(solution)/shard_map/while
  127.3 1.9 copy-start.3
  130.5 2.5 %copy-start.6 = (bf16[128,4,4,128]{0,3,2,1:T(8,128)(2,1)S(1)}, bf16[128,4,4,128]{0,3,2,1:T(8,128)(2,1)}, u32[]{:S(2)}) copy-start(bf16[128,4,4,128]{0,3,2,1:T(8,128)(2,1)} %get-tuple-element.565) | copy-start | bytes 1572868 | tf_op jit(solution)/shard_map/while
  133.1 2.2 copy-start.5
  135.2 3.6 %copy-start.1 = (bf16[128,4,4,128]{0,3,2,1:T(8,128)(2,1)S(1)}, bf16[128,4,4,128]{0,3,2,1:T(8,128)(2,1)}, u32[]{:S(2)}) copy-start(bf16[128,4,4,128]{0,3,2,1:T(8,128)(2,1)} %get-tuple-element.562) | copy-start | bytes 1572868 | tf_op jit(solution)/shard_map/while
  137.8 2.6 %copy-start.2 = (bf16[2,1024,1024]{1,2,0:T(8,128)(2,1)S(1)}, bf16[2,1024,1024]{1,2,0:T(8,128)(2,1)}, u32[]{:S(2)}) copy-start(bf16[2,1024,1024]{1,2,0:T(8,128)(2,1)} %get-tuple-element.541) | copy-start | bytes 12582916 | tf_op jit(solution)/shard_map/while
  140.7 1.9 copy-start.3
Sparse Core Ops, SparseCore 0:
  9.5 23.9 all-gather.4
  36.3 50.7 all-gather.2
  149.0 71.7 reduce-scatter.1
